TPU v7x, 32 devices: a whole 2x2x4 slice. The times are simulated.
32 devices in a mesh: row: 4 (over y, x), col: 2 (over core), depth: 4 (over z).
Axes of the slice: x: 2, y: 2, z: 4, core: 2. Of those that a mesh axis runs over, the one named last changes fastest.
Arguments:
- a_cols: float32 [4096, 1024], P(('row', 'col')), may hold values from -16 to 24, as said below
- past_panels: float32 [4096, 2048], P(('row', 'col'), 'depth'), may hold values from -1 to 1
Outputs:
- factor: float32 [4096, 1024], P(('row', 'col'))
Inputs may be any that keep to these rules, and one draw needn't show every extreme that they name: a_cols minus past_panels times the transpose of the top 1024 rows of past_panels is the first 1024 columns of a symmetric positive definite matrix whose top block has eigenvalues between 2 and 12.
All inputs are finite; a program needn't handle non-finite values.
Results may differ from a plain program's by a relative error of at most 0.0001.
Values sent between devices are 32-bit elements.
A program may use at most 64 MiB of HBM per device.

v0:
```python
import jax
import jax.numpy as jnp
from jax import lax
from jax.sharding import PartitionSpec as P

NB = 512
STEPS = 2


def spread(array, axis, root):
    mine = lax.axis_index(axis) == root
    return lax.psum(jnp.where(mine, array, jnp.zeros_like(array)), axis)


def outer_rows(left, right):
    return lax.dot_general(
        left,
        right,
        (((1,), (1,)), ((), ())),
        precision=lax.Precision.HIGHEST,
        preferred_element_type=jnp.float32,
    )


def body(a_cols, past_panels):
    local_rows = a_cols.shape[0]
    position = lax.axis_index(("row", "col"))
    row_ids = position * local_rows + lax.broadcasted_iota(jnp.int32, (local_rows, NB), 0)
    col_ids = lax.broadcasted_iota(jnp.int32, (local_rows, NB), 1)
    result = jnp.zeros(a_cols.shape, jnp.float32)
    for section in range(STEPS):
        start = section * NB
        root = start // local_rows
        above = spread(past_panels, ("row", "col"), root)
        partial_value = outer_rows(past_panels, above)
        if section > 0:
            layer = lax.axis_index("depth")
            owned_ids = [layer + 0]
            owned_cols = [
                lax.dynamic_slice_in_dim(result, jnp.minimum(index, section - 1) * NB, NB, 1)
                for index in owned_ids
            ]
            sent_rows = jnp.stack([block for block in owned_cols])
            got_rows = spread(sent_rows, ("row", "col"), root)
            weight = (owned_ids[0] < section).astype(jnp.float32)
            partial_value = partial_value + weight * outer_rows(owned_cols[0], got_rows[0])
        summed = lax.psum(partial_value, "depth")
        update = a_cols[:, start : start + NB] - summed
        block = spread(update, ("row", "col"), root)
        diag_factor = jnp.linalg.cholesky(block)
        solved = jax.scipy.linalg.solve_triangular(diag_factor, update.T, lower=True).T
        new_panel = jnp.where(row_ids >= start + col_ids, solved, jnp.float32(0.0))
        result = result.at[:, start : start + NB].set(new_panel)
    return result


def solution(mesh):
    in_specs = (P(("row", "col"), None), P(("row", "col"), "depth"))
    out_specs = P(("row", "col"), None)
    return jax.shard_map(body, mesh=mesh, in_specs=in_specs, out_specs=out_specs, check_vma=False)
```

profile of v0, /device:TPU:0, one launch (start us, length us, event | category | flops | bytes accessed | tf_op | source)
XLA Modules:
  0.0 672.5 jit_solution(3477876616623234303)
XLA Ops:
  6.5 1.6 copy.4
  8.1 1.7 broadcast_select_fusion.3
  9.8 60.1 %all-reduce.10.cloned.1.call-done = f32[512,512]{0,1:T(8,128)} async-done(((f32[512,512]{0,1:T(8,128)}), f32[512,512]{0,1:T(8,128)}) %all-reduce.10.cloned.1.call-update) | async-done | bytes 1048592 | tf_op jit(solution)/shard_map/psum | solution.py:12
  69.9 5.7 convolution_bitcast_fusion.1
  75.7 2.7 fusion.69
  78.8 48.2 %all-reduce.12.cloned.1.call-done = f32[512,512]{0,1:T(8,128)} async-done(((f32[512,512]{0,1:T(8,128)}), f32[512,512]{0,1:T(8,128)}) %all-reduce.12.cloned.1.call-update) | async-done | bytes 1048592 | tf_op jit(solution)/shard_map/psum | solution.py:47
  127.0 2.8 broadcast_select_fusion.2
  129.9 1.0 compare_reduce_fusion.8
  130.8 55.3 %all-reduce.14.cloned.1.call-done = f32[512,512]{0,1:T(8,128)} async-done(((f32[512,512]{0,1:T(8,128)}), f32[512,512]{0,1:T(8,128)}) %all-reduce.14.cloned.1.call-update) | async-done | bytes 1048592 | tf_op jit(solution)/shard_map/psum | solution.py:12
  186.1 1.6 copy.5
  188.0 1.0 copy-done.7
  189.0 11.7 %cholesky.286 = f32[128,128]{1,0:T(8,128)S(1)} custom-call(f32[128,128]{1,0:T(8,128)S(1)} %cholesky.426), custom_call_target="Cholesky" | custom-call | tf_op jit(solution)/shard_map/jit(cholesky)/cholesky | solution.py:50
  200.8 9.8 %custom-call.27 = f32[1,128,128]{1,2,0:T(8,128)S(1)} custom-call(f32[1,128,128]{2,1,0:T(8,128)S(1)} %get-tuple-element.96), custom_call_target="InvertDiagBlocksLowerTriangular" | custom-call | tf_op jit(solution)/shard_map/jit(cholesky)/cholesky | solution.py:50
  210.7 1.2 constant_dynamic-update-slice_fusion.5
  212.0 1.3 convolution_subtract_fusion.7
  213.2 11.7 %cholesky.305 = f32[128,128]{1,0:T(8,128)S(1)} custom-call(f32[128,128]{1,0:T(8,128)S(1)} %cholesky.430), custom_call_target="Cholesky" | custom-call | tf_op jit(solution)/shard_map/jit(cholesky)/cholesky | solution.py:50
  225.0 10.3 %custom-call.28 = f32[1,128,128]{1,2,0:T(8,128)S(1)} custom-call(f32[1,128,128]{2,1,0:T(8,128)S(1)} %get-tuple-element.93), custom_call_target="InvertDiagBlocksLowerTriangular" | custom-call | tf_op jit(solution)/shard_map/jit(cholesky)/cholesky | solution.py:50
  235.6 1.3 convolution_subtract_fusion.9
  236.9 11.7 %cholesky.326 = f32[128,128]{1,0:T(8,128)S(1)} custom-call(f32[128,128]{1,0:T(8,128)S(1)} %cholesky.435), custom_call_target="Cholesky" | custom-call | tf_op jit(solution)/shard_map/jit(cholesky)/cholesky | solution.py:50
  249.2 9.8 %custom-call.29 = f32[1,128,128]{1,2,0:T(8,128)S(1)} custom-call(f32[1,128,128]{2,1,0:T(8,128)S(1)} %get-tuple-element.90), custom_call_target="InvertDiagBlocksLowerTriangular" | custom-call | tf_op jit(solution)/shard_map/jit(cholesky)/cholesky | solution.py:50
  259.3 1.2 convolution_subtract_fusion.11
  260.5 11.7 %cholesky.343 = f32[128,128]{1,0:T(8,128)S(1)} custom-call(f32[128,128]{1,0:T(8,128)S(1)} %convolution_subtract_fusion.11), custom_call_target="Cholesky" | custom-call | tf_op jit(solution)/shard_map/jit(cholesky)/cholesky | solution.py:50
  276.0 1.3 select_select_fusion.1
  277.3 11.1 %while.6 = (s32[]{:T(128)}, f32[512,512]{1,0:T(8,128)}, s32[4,2]{0,1:T(2,128)S(1)}, f32[4,128,128]{2,1,0:T(8,128)S(1)}, s32[]{:T(128)}) while((s32[]{:T(128)}, f32[512,512]{1,0:T(8,128)}, s32[4,2]{0,1:T(2,128)S(1)}, f32[4,128,128]{2,1,0:T(8,128)S(1)}, s32[]{:T(128)}) %tuple.63), condition=%wide.while_cond.2, body=%wide.while_body.2.sunk | while | flops 2 | bytes 131181 | solution.py:51
  278.0 2.2 bitcast_dynamic-update-slice_fusion.4
  280.7 2.2 bitcast_dynamic-update-slice_fusion.4
  283.5 2.2 bitcast_dynamic-update-slice_fusion.4
  286.3 2.1 bitcast_dynamic-update-slice_fusion.4
  288.4 39.3 %custom-call.30 = f32[4,128,128]{1,2,0:T(8,128)S(1)} custom-call(f32[4,128,128]{2,1,0:T(8,128)S(1)} %get-tuple-element.45), custom_call_target="InvertDiagBlocksLowerTriangular" | custom-call | tf_op jit(solution)/shard_map/jit(_solve_triangular)/triangular_solve | solution.py:51
  328.2 1.2 convolution_subtract_fusion.3
  329.8 1.3 convolution_subtract_fusion.2
  331.6 1.6 convolution_subtract_fusion.5
  333.6 0.7 fusion.2
  334.3 1.2 fusion.6
  335.6 61.2 %all-reduce.20.cloned.1.call-done = (f32[512,512]{0,1:T(8,128)}, f32[512,512]{0,1:T(8,128)}) async-done(((f32[512,512]{0,1:T(8,128)}, f32[512,512]{0,1:T(8,128)}), (f32[512,512]{0,1:T(8,128)}, f32[512,512]{0,1:T(8,128)})) %all-reduce.20.cloned.1.call-update) | async-done | bytes 2097168 | tf_op jit(solution)/shard_map/psum | solution.py:12
  396.8 4.8 convolution_bitcast_fusion
  401.6 2.9 fusion
  405.1 50.5 %all-reduce.16.cloned.1.call-done = f32[512,512]{0,1:T(8,128)} async-done(((f32[512,512]{0,1:T(8,128)}), f32[512,512]{0,1:T(8,128)}) %all-reduce.16.cloned.1.call-update) | async-done | bytes 1048592 | tf_op jit(solution)/shard_map/psum | solution.py:47
  455.6 2.8 broadcast_select_fusion
  458.4 56.2 %all-reduce.18.cloned.1.call-done = f32[512,512]{0,1:T(8,128)} async-done(((f32[512,512]{0,1:T(8,128)}), f32[512,512]{0,1:T(8,128)}) %all-reduce.18.cloned.1.call-update) | async-done | bytes 1048592 | tf_op jit(solution)/shard_map/psum | solution.py:12
  514.6 1.6 copy.9
  516.5 1.0 copy-done.6
  517.5 11.7 %cholesky.358 = f32[128,128]{1,0:T(8,128)S(1)} custom-call(f32[128,128]{1,0:T(8,128)S(1)} %cholesky.439), custom_call_target="Cholesky" | custom-call | tf_op jit(solution)/shard_map/jit(cholesky)/cholesky | solution.py:50
  529.4 9.8 %custom-call.31 = f32[1,128,128]{1,2,0:T(8,128)S(1)} custom-call(f32[1,128,128]{2,1,0:T(8,128)S(1)} %get-tuple-element.86), custom_call_target="InvertDiagBlocksLowerTriangular" | custom-call | tf_op jit(solution)/shard_map/jit(cholesky)/cholesky | solution.py:50
  539.2 1.2 constant_dynamic-update-slice_fusion.3
  540.4 1.3 convolution_subtract_fusion.6
  541.7 11.7 %cholesky.377 = f32[128,128]{1,0:T(8,128)S(1)} custom-call(f32[128,128]{1,0:T(8,128)S(1)} %cholesky.443), custom_call_target="Cholesky" | custom-call | tf_op jit(solution)/shard_map/jit(cholesky)/cholesky | solution.py:50
  554.8 10.2 %custom-call.32 = f32[1,128,128]{1,2,0:T(8,128)S(1)} custom-call(f32[1,128,128]{2,1,0:T(8,128)S(1)} %get-tuple-element.83), custom_call_target="InvertDiagBlocksLowerTriangular" | custom-call | tf_op jit(solution)/shard_map/jit(cholesky)/cholesky | solution.py:50
  565.3 1.3 convolution_subtract_fusion.8
  566.6 11.7 %cholesky.398 = f32[128,128]{1,0:T(8,128)S(1)} custom-call(f32[128,128]{1,0:T(8,128)S(1)} %cholesky.448), custom_call_target="Cholesky" | custom-call | tf_op jit(solution)/shard_map/jit(cholesky)/cholesky | solution.py:50
  579.0 9.8 %custom-call.33 = f32[1,128,128]{1,2,0:T(8,128)S(1)} custom-call(f32[1,128,128]{2,1,0:T(8,128)S(1)} %get-tuple-element.80), custom_call_target="InvertDiagBlocksLowerTriangular" | custom-call | tf_op jit(solution)/shard_map/jit(cholesky)/cholesky | solution.py:50
  589.0 1.2 convolution_subtract_fusion.10
  590.3 11.8 %cholesky.415 = f32[128,128]{1,0:T(8,128)S(1)} custom-call(f32[128,128]{1,0:T(8,128)S(1)} %convolution_subtract_fusion.10), custom_call_target="Cholesky" | custom-call | tf_op jit(solution)/shard_map/jit(cholesky)/cholesky | solution.py:50
  605.3 1.1 select_select_fusion
  606.4 11.7 %while.7 = (s32[]{:T(128)}, f32[512,512]{1,0:T(8,128)}, s32[4,2]{0,1:T(2,128)S(1)}, f32[4,128,128]{2,1,0:T(8,128)S(1)}, s32[]{:T(128)}) while((s32[]{:T(128)}, f32[512,512]{1,0:T(8,128)}, s32[4,2]{0,1:T(2,128)S(1)}, f32[4,128,128]{2,1,0:T(8,128)S(1)}, s32[]{:T(128)}) %tuple.82), condition=%wide.while_cond.2.clone, body=%wide.while_body.2.clone.sunk | while | flops 2 | bytes 131181 | solution.py:51
  607.1 2.3 bitcast_dynamic-update-slice_fusion.5
  610.0 2.3 bitcast_dynamic-update-slice_fusion.5
  613.0 2.3 bitcast_dynamic-update-slice_fusion.5
  615.9 2.2 bitcast_dynamic-update-slice_fusion.5
  618.1 39.3 %custom-call.34 = f32[4,128,128]{1,2,0:T(8,128)S(1)} custom-call(f32[4,128,128]{2,1,0:T(8,128)S(1)} %get-tuple-element.46), custom_call_target="InvertDiagBlocksLowerTriangular" | custom-call | tf_op jit(solution)/shard_map/jit(_solve_triangular)/triangular_solve | solution.py:51
  657.9 1.2 convolution_subtract_fusion.1
  659.5 1.3 convolution_subtract_fusion
  661.3 1.6 convolution_subtract_fusion.4
  663.6 1.8 copy.10
  (91 shorter events, 16.6 us)
Async XLA Ops:
  6.5 63.4 %all-reduce.10.cloned.1.call-start = ((), (), s32[]{:S(2)}) async-start(), calls=%async_computation | async-start | bytes 2097152 | tf_op jit(solution)/shard_map/psum | solution.py:12
  8.1 61.8 %copy-start = (f32[512,512]{1,0:T(8,128)S(1)}, f32[512,512]{1,0:T(8,128)}, u32[]{:S(2)}) copy-start(f32[512,512]{1,0:T(8,128)} %param.10) | copy-start | bytes 3145732
  9.8 117.2 %all-reduce.12.cloned.1.call-start = ((), (), s32[]{:S(2)}) async-start(), calls=%async_computation.1 | async-start | bytes 2097152 | tf_op jit(solution)/shard_map/psum | solution.py:47
  75.7 110.4 %all-reduce.14.cloned.1.call-start = ((), (), s32[]{:S(2)}) async-start(), calls=%async_computation.2 | async-start | bytes 2097152 | tf_op jit(solution)/shard_map/psum | solution.py:12
  129.8 267.0 %all-reduce.20.cloned.1.call-start = ((), (), s32[]{:S(2)}) async-start(), calls=%async_computation.5 | async-start | bytes 4194304 | tf_op jit(solution)/shard_map/psum | solution.py:12
  186.1 1.7 copy-start.1
  188.0 1.0 copy-start.7
  236.9 90.9 %copy-start.3 = (f32[512,512]{1,0:T(8,128)S(1)}, f32[512,512]{1,0:T(8,128)}, u32[]{:S(2)}) copy-start(f32[512,512]{1,0:T(8,128)} %get-tuple-element.72) | copy-start | bytes 3145732
  335.5 120.1 %all-reduce.16.cloned.1.call-start = ((), (), s32[]{:S(2)}) async-start(), calls=%async_computation.3 | async-start | bytes 2097152 | tf_op jit(solution)/shard_map/psum | solution.py:47
  396.8 4.8 copy-start.8
  401.6 3.2 copy-start.5
  404.5 110.1 %all-reduce.18.cloned.1.call-start = ((), (), s32[]{:S(2)}) async-start(), calls=%async_computation.4 | async-start | bytes 2097152 | tf_op jit(solution)/shard_map/psum | solution.py:12
  514.6 1.7 copy-start.2
  516.5 1.0 copy-start.6
  566.6 90.9 %copy-start.4 = (f32[512,512]{1,0:T(8,128)S(1)}, f32[512,512]{1,0:T(8,128)}, u32[]{:S(2)}) copy-start(f32[512,512]{1,0:T(8,128)} %get-tuple-element.70) | copy-start | bytes 3145732
Sparse Core Ops, SparseCore 0:
  10.5 59.4 all-reduce.9
  75.8 51.1 all-reduce.11
  130.1 55.9 all-reduce.13
  335.6 61.0 all-reduce.19
  404.6 50.9 all-reduce.15
  458.6 55.9 all-reduce.17
where the time goes:
time: 678 us; the launch traced here: 672 us
  waiting for transfers between devices  332 us (49%)
  other arithmetic  250 us (37%)
  matrix products  35.9 us (5%)
  local copies, waits for them, and re-layouts  34.9 us (5%)
  between operations  19.2 us (3%)
    psum x4, waiting for transfers between devices, spread(): return lax.psum(jnp.where(mine, array, jnp.zeros_like(array)), axis)  233 us
    another operation x29, other arithmetic, body(): diag_factor = jnp.linalg.cholesky(block)  158 us
    psum x2, waiting for transfers between devices, body(): summed = lax.psum(partial_value, 'depth')  98.7 us
    another operation x5, other arithmetic, body(): jax.scipy.linalg.solve_triangular(diag_factor, update.T, lower=True)  81 us
    another operation x27, local copies, waits for them, and re-layouts, body(): jax.scipy.linalg.solve_triangular(diag_factor, update.T, lower=True)  22.6 us
  transfers between devices with their start and end apart: 6, of which 6 were waited for; matrix products, arithmetic and copies ran while one was open for 1% of the time, Pallas kernels for 0%

commit v1 on v0

--- a/solution.py
+++ b/solution.py
@@ -44,7 +44,7 @@
             got_rows = spread(sent_rows, ("row", "col"), root)
             weight = (owned_ids[0] < section).astype(jnp.float32)
             partial_value = partial_value + weight * outer_rows(owned_cols[0], got_rows[0])
-        summed = lax.psum(partial_value, "depth")
+        summed = jnp.sum(lax.all_gather(partial_value, "depth"), axis=0)
         update = a_cols[:, start : start + NB] - summed
         block = spread(update, ("row", "col"), root)
         diag_factor = jnp.linalg.cholesky(block)

time: 678 us -> 755 us (1.11)
  waiting for transfers between devices: 332 us -> 387 us
  local copies, waits for them, and re-layouts: 34.9 us -> 47.7 us
    all_gather x0 -> x2, waiting for transfers between devices: none -> 157 us  [body(): summed = jnp.sum(lax.all_gather(partial_value, 'depth'), axis=0)]
    psum x2 -> x0, waiting for transfers between devices: 98.7 us -> none  [body(): summed = lax.psum(partial_value, 'depth')]
    all_gather x0 -> x2, local copies, waits for them, and re-layouts: none -> 12.4 us  [body(): summed = jnp.sum(lax.all_gather(partial_value, 'depth'), axis=0)]
    reduce_sum x0 -> x2, other arithmetic: none -> 9.36 us  [body(): summed = jnp.sum(lax.all_gather(partial_value, 'depth'), axis=0)]
where the time goes in v1:
time: 755 us; the launch traced here: 748 us
  waiting for transfers between devices  387 us (51%)
  other arithmetic  257 us (34%)
  local copies, waits for them, and re-layouts  47.7 us (6%)
  matrix products  35.8 us (5%)
  between operations  19.2 us (3%)
    psum x4, waiting for transfers between devices, spread(): return lax.psum(jnp.where(mine, array, jnp.zeros_like(array)), axis)  231 us
    another operation x29, other arithmetic, body(): diag_factor = jnp.linalg.cholesky(block)  158 us
    all_gather x2, waiting for transfers between devices, body(): summed = jnp.sum(lax.all_gather(partial_value, 'depth'), axis=0)  157 us
    another operation x5, other arithmetic, body(): jax.scipy.linalg.solve_triangular(diag_factor, update.T, lower=True)  81.1 us
    another operation x27, local copies, waits for them, and re-layouts, body(): jax.scipy.linalg.solve_triangular(diag_factor, update.T, lower=True)  23 us
  transfers between devices with their start and end apart: 6, of which 6 were waited for; matrix products, arithmetic and copies ran while one was open for 1% of the time, Pallas kernels for 0%

profile of v1, /device:TPU:0, one launch (start us, length us, event | category | flops | bytes accessed | tf_op | source)
XLA Modules:
  0.0 747.7 jit_solution(5471993620824718786)
XLA Ops:
  6.5 1.6 copy.4
  8.1 1.7 broadcast_select_fusion.3
  9.9 60.0 %all-reduce.8.cloned.1.call-done = f32[512,512]{0,1:T(8,128)} async-done(((f32[512,512]{0,1:T(8,128)}), f32[512,512]{0,1:T(8,128)}) %all-reduce.8.cloned.1.call-update) | async-done | bytes 1048592 | tf_op jit(solution)/shard_map/psum | solution.py:12
  69.9 5.7 convolution_bitcast_fusion.1
  75.7 2.7 fusion.69
  78.7 77.1 %all-gather.5.cloned.1.call-done = f32[2048,512]{0,1:T(8,128)} async-done(((f32[512,512]{0,1:T(8,128)}), f32[2048,512]{0,1:T(8,128)}) %all-gather.5.cloned.1.call-update) | async-done | bytes 4194320 | tf_op jit(solution)/shard_map/all_gather | solution.py:47
  155.8 6.0 reshape.104
  161.8 4.7 reduce_sum.18
  166.5 1.7 broadcast_select_fusion.2
  169.3 54.2 %all-reduce.10.cloned.1.call-done = f32[512,512]{0,1:T(8,128)} async-done(((f32[512,512]{0,1:T(8,128)}), f32[512,512]{0,1:T(8,128)}) %all-reduce.10.cloned.1.call-update) | async-done | bytes 1048592 | tf_op jit(solution)/shard_map/psum | solution.py:12
  223.5 1.6 copy.5
  226.4 11.7 %cholesky.286 = f32[128,128]{1,0:T(8,128)S(1)} custom-call(f32[128,128]{1,0:T(8,128)S(1)} %cholesky.426), custom_call_target="Cholesky" | custom-call | tf_op jit(solution)/shard_map/jit(cholesky)/cholesky | solution.py:50
  238.2 9.8 %custom-call.27 = f32[1,128,128]{1,2,0:T(8,128)S(1)} custom-call(f32[1,128,128]{2,1,0:T(8,128)S(1)} %get-tuple-element.96), custom_call_target="InvertDiagBlocksLowerTriangular" | custom-call | tf_op jit(solution)/shard_map/jit(cholesky)/cholesky | solution.py:50
  248.1 1.2 constant_dynamic-update-slice_fusion.5
  249.4 1.3 convolution_subtract_fusion.7
  250.7 11.7 %cholesky.305 = f32[128,128]{1,0:T(8,128)S(1)} custom-call(f32[128,128]{1,0:T(8,128)S(1)} %cholesky.430), custom_call_target="Cholesky" | custom-call | tf_op jit(solution)/shard_map/jit(cholesky)/cholesky | solution.py:50
  262.4 10.0 %custom-call.28 = f32[1,128,128]{1,2,0:T(8,128)S(1)} custom-call(f32[1,128,128]{2,1,0:T(8,128)S(1)} %get-tuple-element.93), custom_call_target="InvertDiagBlocksLowerTriangular" | custom-call | tf_op jit(solution)/shard_map/jit(cholesky)/cholesky | solution.py:50
  272.6 1.3 convolution_subtract_fusion.9
  273.9 11.7 %cholesky.326 = f32[128,128]{1,0:T(8,128)S(1)} custom-call(f32[128,128]{1,0:T(8,128)S(1)} %cholesky.435), custom_call_target="Cholesky" | custom-call | tf_op jit(solution)/shard_map/jit(cholesky)/cholesky | solution.py:50
  286.3 9.8 %custom-call.29 = f32[1,128,128]{1,2,0:T(8,128)S(1)} custom-call(f32[1,128,128]{2,1,0:T(8,128)S(1)} %get-tuple-element.90), custom_call_target="InvertDiagBlocksLowerTriangular" | custom-call | tf_op jit(solution)/shard_map/jit(cholesky)/cholesky | solution.py:50
  296.4 1.2 convolution_subtract_fusion.11
  297.6 11.7 %cholesky.343 = f32[128,128]{1,0:T(8,128)S(1)} custom-call(f32[128,128]{1,0:T(8,128)S(1)} %convolution_subtract_fusion.11), custom_call_target="Cholesky" | custom-call | tf_op jit(solution)/shard_map/jit(cholesky)/cholesky | solution.py:50
  313.0 1.4 select_select_fusion.1
  314.4 11.4 %while.6 = (s32[]{:T(128)}, f32[512,512]{1,0:T(8,128)}, s32[4,2]{0,1:T(2,128)S(1)}, f32[4,128,128]{2,1,0:T(8,128)S(1)}, s32[]{:T(128)}) while((s32[]{:T(128)}, f32[512,512]{1,0:T(8,128)}, s32[4,2]{0,1:T(2,128)S(1)}, f32[4,128,128]{2,1,0:T(8,128)S(1)}, s32[]{:T(128)}) %tuple.63), condition=%wide.while_cond.2, body=%wide.while_body.2.sunk | while | flops 2 | bytes 131181 | solution.py:51
  315.1 2.2 bitcast_dynamic-update-slice_fusion.4
  317.9 2.2 bitcast_dynamic-update-slice_fusion.4
  320.8 2.2 bitcast_dynamic-update-slice_fusion.4
  323.7 2.2 bitcast_dynamic-update-slice_fusion.4
  325.8 39.3 %custom-call.30 = f32[4,128,128]{1,2,0:T(8,128)S(1)} custom-call(f32[4,128,128]{2,1,0:T(8,128)S(1)} %get-tuple-element.45), custom_call_target="InvertDiagBlocksLowerTriangular" | custom-call | tf_op jit(solution)/shard_map/jit(_solve_triangular)/triangular_solve | solution.py:51
  365.6 1.2 convolution_subtract_fusion.3
  367.2 1.3 convolution_subtract_fusion.2
  369.0 1.6 convolution_subtract_fusion.5
  371.7 1.2 fusion.6
  372.9 61.2 %all-reduce.14.cloned.1.call-done = (f32[512,512]{0,1:T(8,128)}, f32[512,512]{0,1:T(8,128)}) async-done(((f32[512,512]{0,1:T(8,128)}, f32[512,512]{0,1:T(8,128)}), (f32[512,512]{0,1:T(8,128)}, f32[512,512]{0,1:T(8,128)})) %all-reduce.14.cloned.1.call-update) | async-done | bytes 2097168 | tf_op jit(solution)/shard_map/psum | solution.py:12
  434.1 4.8 convolution_bitcast_fusion
  439.0 2.9 fusion
  442.3 79.5 %all-gather.7.cloned.1.call-done = f32[2048,512]{0,1:T(8,128)} async-done(((f32[512,512]{0,1:T(8,128)}), f32[2048,512]{0,1:T(8,128)}) %all-gather.7.cloned.1.call-update) | async-done | bytes 4194320 | tf_op jit(solution)/shard_map/all_gather | solution.py:47
  521.8 6.4 reshape.105
  528.2 4.7 reduce_sum.19
  532.9 1.6 broadcast_select_fusion
  534.6 55.3 %all-reduce.12.cloned.1.call-done = f32[512,512]{0,1:T(8,128)} async-done(((f32[512,512]{0,1:T(8,128)}), f32[512,512]{0,1:T(8,128)}) %all-reduce.12.cloned.1.call-update) | async-done | bytes 1048592 | tf_op jit(solution)/shard_map/psum | solution.py:12
  589.9 1.6 copy.9
  592.8 11.7 %cholesky.358 = f32[128,128]{1,0:T(8,128)S(1)} custom-call(f32[128,128]{1,0:T(8,128)S(1)} %cholesky.439), custom_call_target="Cholesky" | custom-call | tf_op jit(solution)/shard_map/jit(cholesky)/cholesky | solution.py:50
  604.7 9.8 %custom-call.31 = f32[1,128,128]{1,2,0:T(8,128)S(1)} custom-call(f32[1,128,128]{2,1,0:T(8,128)S(1)} %get-tuple-element.86), custom_call_target="InvertDiagBlocksLowerTriangular" | custom-call | tf_op jit(solution)/shard_map/jit(cholesky)/cholesky | solution.py:50
  614.5 1.2 constant_dynamic-update-slice_fusion.3
  615.7 1.3 convolution_subtract_fusion.6
  617.0 11.9 %cholesky.377 = f32[128,128]{1,0:T(8,128)S(1)} custom-call(f32[128,128]{1,0:T(8,128)S(1)} %cholesky.443), custom_call_target="Cholesky" | custom-call | tf_op jit(solution)/shard_map/jit(cholesky)/cholesky | solution.py:50
  630.3 9.8 %custom-call.32 = f32[1,128,128]{1,2,0:T(8,128)S(1)} custom-call(f32[1,128,128]{2,1,0:T(8,128)S(1)} %get-tuple-element.83), custom_call_target="InvertDiagBlocksLowerTriangular" | custom-call | tf_op jit(solution)/shard_map/jit(cholesky)/cholesky | solution.py:50
  640.3 1.3 convolution_subtract_fusion.8
  641.7 11.7 %cholesky.398 = f32[128,128]{1,0:T(8,128)S(1)} custom-call(f32[128,128]{1,0:T(8,128)S(1)} %cholesky.448), custom_call_target="Cholesky" | custom-call | tf_op jit(solution)/shard_map/jit(cholesky)/cholesky | solution.py:50
  654.1 9.8 %custom-call.33 = f32[1,128,128]{1,2,0:T(8,128)S(1)} custom-call(f32[1,128,128]{2,1,0:T(8,128)S(1)} %get-tuple-element.80), custom_call_target="InvertDiagBlocksLowerTriangular" | custom-call | tf_op jit(solution)/shard_map/jit(cholesky)/cholesky | solution.py:50
  664.1 1.2 convolution_subtract_fusion.10
  665.3 11.9 %cholesky.415 = f32[128,128]{1,0:T(8,128)S(1)} custom-call(f32[128,128]{1,0:T(8,128)S(1)} %convolution_subtract_fusion.10), custom_call_target="Cholesky" | custom-call | tf_op jit(solution)/shard_map/jit(cholesky)/cholesky | solution.py:50
  680.5 1.1 select_select_fusion
  681.6 11.7 %while.7 = (s32[]{:T(128)}, f32[512,512]{1,0:T(8,128)}, s32[4,2]{0,1:T(2,128)S(1)}, f32[4,128,128]{2,1,0:T(8,128)S(1)}, s32[]{:T(128)}) while((s32[]{:T(128)}, f32[512,512]{1,0:T(8,128)}, s32[4,2]{0,1:T(2,128)S(1)}, f32[4,128,128]{2,1,0:T(8,128)S(1)}, s32[]{:T(128)}) %tuple.82), condition=%wide.while_cond.2.clone, body=%wide.while_body.2.clone.sunk | while | flops 2 | bytes 131181 | solution.py:51
  682.3 2.3 bitcast_dynamic-update-slice_fusion.5
  685.2 2.3 bitcast_dynamic-update-slice_fusion.5
  688.1 2.3 bitcast_dynamic-update-slice_fusion.5
  691.1 2.2 bitcast_dynamic-update-slice_fusion.5
  693.3 39.3 %custom-call.34 = f32[4,128,128]{1,2,0:T(8,128)S(1)} custom-call(f32[4,128,128]{2,1,0:T(8,128)S(1)} %get-tuple-element.46), custom_call_target="InvertDiagBlocksLowerTriangular" | custom-call | tf_op jit(solution)/shard_map/jit(_solve_triangular)/triangular_solve | solution.py:51
  733.0 1.2 convolution_subtract_fusion.1
  734.7 1.3 convolution_subtract_fusion
  736.5 1.6 convolution_subtract_fusion.4
  738.8 1.8 copy.10
  (95 shorter events, 20.2 us)
Async XLA Ops:
  6.5 63.4 %all-reduce.8.cloned.1.call-start = ((), (), s32[]{:S(2)}) async-start(), calls=%async_computation | async-start | bytes 2097152 | tf_op jit(solution)/shard_map/psum | solution.py:12
  8.1 61.8 %copy-start = (f32[512,512]{1,0:T(8,128)S(1)}, f32[512,512]{1,0:T(8,128)}, u32[]{:S(2)}) copy-start(f32[512,512]{1,0:T(8,128)} %param.10) | copy-start | bytes 3145732
  9.9 145.9 %all-gather.5.cloned.1.call-start = ((), (), s32[]{:S(2)}) async-start(), calls=%async_computation.3 | async-start | bytes 5242880 | tf_op jit(solution)/shard_map/all_gather | solution.py:47
  75.6 147.9 %all-reduce.10.cloned.1.call-start = ((), (), s32[]{:S(2)}) async-start(), calls=%async_computation.1 | async-start | bytes 2097152 | tf_op jit(solution)/shard_map/psum | solution.py:12
  168.2 266.0 %all-reduce.14.cloned.1.call-start = ((), (), s32[]{:S(2)}) async-start(), calls=%async_computation.5 | async-start | bytes 4194304 | tf_op jit(solution)/shard_map/psum | solution.py:12
  223.5 1.7 copy-start.1
  225.4 1.0 copy-start.7
  273.9 91.2 %copy-start.3 = (f32[512,512]{1,0:T(8,128)S(1)}, f32[512,512]{1,0:T(8,128)}, u32[]{:S(2)}) copy-start(f32[512,512]{1,0:T(8,128)} %get-tuple-element.72) | copy-start | bytes 3145732
  372.9 148.9 %all-gather.7.cloned.1.call-start = ((), (), s32[]{:S(2)}) async-start(), calls=%async_computation.4 | async-start | bytes 5242880 | tf_op jit(solution)/shard_map/all_gather | solution.py:47
  434.1 4.8 copy-start.8
  438.9 3.0 copy-start.5
  441.9 148.0 %all-reduce.12.cloned.1.call-start = ((), (), s32[]{:S(2)}) async-start(), calls=%async_computation.2 | async-start | bytes 2097152 | tf_op jit(solution)/shard_map/psum | solution.py:12
  589.9 1.7 copy-start.2
  591.8 1.0 copy-start.6
  641.6 91.0 %copy-start.4 = (f32[512,512]{1,0:T(8,128)S(1)}, f32[512,512]{1,0:T(8,128)}, u32[]{:S(2)}) copy-start(f32[512,512]{1,0:T(8,128)} %get-tuple-element.70) | copy-start | bytes 3145732
Sparse Core Ops, SparseCore 0:
  10.5 59.4 all-reduce.7
  75.8 79.9 all-gather.4
  168.3 55.1 all-reduce.9
  373.0 61.0 all-reduce.13
  442.0 79.7 all-gather.6
  534.7 55.1 all-reduce.11
